TPU v7x, 32 devices: a whole 2x2x4 slice. The times are simulated.
32 devices in a mesh: nodes: 32 (over z, y, x, core).
Axes of the slice: x: 2, y: 2, z: 4, core: 2. Of those that a mesh axis runs over, the one named last changes fastest.
Arguments:
- adjacency: bfloat16 [16384, 16384], P('nodes')
- features: bfloat16 [16384, 602], P('nodes')
- w_one: float32 [602, 256], replicated
- w_two: float32 [256, 41], replicated
- labels: int32 [16384], P('nodes')
- label_mask: int32 [16384], P('nodes')
Outputs:
- output 1: float32 [1], replicated
- output 2: float32 [602, 256], replicated
- output 3: float32 [256, 41], replicated
All inputs are finite; a program needn't handle non-finite values.
Results may differ from a plain program's by a relative error of at most 0.001.
Values are sent between devices in bfloat16 or wider.
A program may use at most 1 GiB of HBM per device.

v0:
```python
import jax
import jax.numpy as jnp
from jax import lax
from jax.sharding import PartitionSpec as P

ROW_CONTRACT = (((0,), (0,)), ((), ()))
COL_CONTRACT = (((1,), (1,)), ((), ()))


def solution(mesh):
    axis_name = 'nodes'

    def local_step(adj_rows, feat_rows, w_one, w_two, label_rows, mask_rows):
        weight_one = w_one.astype(jnp.bfloat16)
        weight_two = w_two.astype(jnp.bfloat16)
        num_classes = w_two.shape[1]
        feats_all = lax.all_gather(feat_rows, axis_name, tiled=True)
        agg_one = jnp.dot(adj_rows, feats_all, preferred_element_type=jnp.float32).astype(jnp.bfloat16)
        pre_one = jnp.dot(agg_one, weight_one, preferred_element_type=jnp.float32)
        hidden = jnp.maximum(pre_one, 0.0).astype(jnp.bfloat16)
        hidden_all = lax.all_gather(hidden, axis_name, tiled=True)
        agg_two = jnp.dot(adj_rows, hidden_all, preferred_element_type=jnp.float32).astype(jnp.bfloat16)
        logits = jnp.dot(agg_two, weight_two, preferred_element_type=jnp.float32)
        weight = mask_rows.astype(jnp.float32)
        label_count = lax.psum(jnp.sum(weight), axis_name)
        onehot = (label_rows[:, None] == jnp.arange(num_classes)[None, :]).astype(jnp.float32)
        log_prob = jax.nn.log_softmax(logits, axis=-1)
        loss_sum = lax.psum(-jnp.sum(weight * jnp.sum(onehot * log_prob, axis=-1)), axis_name)
        grad_two = (weight[:, None] * (jnp.exp(log_prob) - onehot) / label_count).astype(jnp.bfloat16)
        dw_two = lax.psum(lax.dot_general(agg_two, grad_two, ROW_CONTRACT, preferred_element_type=jnp.float32), axis_name)
        back_two = lax.dot_general(grad_two, weight_two, COL_CONTRACT, preferred_element_type=jnp.float32).astype(jnp.bfloat16)
        part_sums = lax.dot_general(adj_rows, back_two, ROW_CONTRACT, preferred_element_type=jnp.float32)
        d_hidden = lax.psum_scatter(part_sums, axis_name, scatter_dimension=0, tiled=True)
        grad_one = jnp.where(pre_one > 0.0, d_hidden, 0.0).astype(jnp.bfloat16)
        dw_one = lax.psum(lax.dot_general(agg_one, grad_one, ROW_CONTRACT, preferred_element_type=jnp.float32), axis_name)
        return ((loss_sum / label_count).reshape(1), dw_one, dw_two)

    return jax.shard_map(local_step, mesh=mesh, in_specs=(P(axis_name, None), P(axis_name, None), P(None, None), P(None, None), P(axis_name), P(axis_name)), out_specs=(P(None), P(None, None), P(None, None)), check_vma=False)
```

profile of v0, /device:TPU:1, one launch (start us, length us, event | category | flops | bytes accessed | tf_op | source)
XLA Modules:
  0.0 646.1 jit_solution(12418597322357213584)
XLA Ops:
  7.2 0.0 all-gather.3.cloned.1.call-start
  7.2 0.7 all-gather.3.cloned.1.call-update
  7.9 0.0 copy-start.1
  7.9 0.0 copy-start.3
  7.9 0.0 all-gather.5.cloned.1.call-start
  8.0 147.8 %all-gather.3.cloned.1.call-done = bf16[16384,602]{0,1:T(8,128)(2,1)} async-done(((bf16[512,602]{0,1:T(8,128)(2,1)}), bf16[16384,602]{0,1:T(8,128)(2,1)}) %all-gather.3.cloned.1.call-update) | async-done | bytes 19726352 | tf_op jit(solution)/shard_map/all_gather | solution.py:17
  155.8 17.0 %convolution_convert_fusion = bf16[512,602]{0,1:T(8,128)(2,1)S(1)} fusion(bf16[512,16384]{1,0:T(8,128)(2,1)} %param.6, bf16[16384,602]{0,1:T(8,128)(2,1)} %all-gather.3.cloned.1.call-done), kind=kOutput, calls=%fused_computation.1 | convolution fusion | flops 10100192256 | bytes 37120000 | tf_op jit(solution)/shard_map/dot_general | solution.py:18
  172.8 0.0 copy-done.1
  172.8 1.1 maximum_convert_fusion
  173.9 0.0 all-gather.5.cloned.1.call-update
  173.9 0.0 reduce-scatter.2.cloned.1.call-start
  174.0 0.0 copy-done.3
  174.0 0.0 copy-start
  174.0 0.0 copy-start.2
  174.0 75.9 %all-gather.5.cloned.1.call-done = bf16[16384,256]{1,0:T(8,128)(2,1)} async-done(((bf16[512,256]{1,0:T(8,128)(2,1)}), bf16[16384,256]{1,0:T(8,128)(2,1)}) %all-gather.5.cloned.1.call-update) | async-done | bytes 8388624 | tf_op jit(solution)/shard_map/all_gather | solution.py:21
  249.9 12.7 %convolution_convert_fusion.2 = bf16[256,512]{1,0:T(8,128)(2,1)S(1)} fusion(bf16[16384,256]{1,0:T(8,128)(2,1)} %all-gather.5.cloned.1.call-done, bf16[512,16384]{1,0:T(8,128)(2,1)} %param.6), kind=kOutput, calls=%fused_computation.3 | convolution fusion | flops 4295098368 | bytes 25427968 | tf_op jit(solution)/shard_map/dot_general | solution.py:22
  262.7 0.0 copy-done
  262.7 0.2 fusion.10
  262.9 0.0 copy-done.2
  263.0 0.6 convert_reduce_fusion
  263.6 38.5 %psum.29 = f32[]{:T(128)} all-reduce(f32[]{:T(128)} %get-tuple-element.3), channel_id=1, replica_groups=mesh['nodes'=32] {'nodes'}, use_global_device_ids=true, to_apply=%region_6.7 | all-reduce | flops 1 | bytes 8 | tf_op jit(solution)/shard_map/psum | solution.py:25
  302.1 14.2 %convolution_bitcast_fusion = f32[16384,256]{1,0:T(8,128)} fusion(bf16[512,16384]{1,0:T(8,128)(2,1)} %param.6, f32[256,41]{0,1:T(8,128)S(1)} %copy-done, f32[512,41]{0,1:T(8,128)S(1)} %get-tuple-element.10, f32[]{:T(128)} %psum.29, f32[512]{0:T(512)S(1)} %convert_element_type.31, f32[512]{0:T(512)S(1)} %log.9, f32[512]{0:T(512)S(1)} %get-tuple-element.9, ...), kind=kOutput, calls=%fused_computation | convolution fusion | flops 4306024448 | bytes 33688580 | tf_op jit(solution)/shard_map/dot_general | solution.py:32
  316.3 0.0 reduce-scatter.2.cloned.1.call-update
  316.3 0.0 all-reduce.3.cloned.1.call-start
  316.4 184.4 %reduce-scatter.2.cloned.1.call-done = f32[512,256]{1,0:T(8,128)} async-done(((f32[16384,256]{1,0:T(8,128)}), f32[512,256]{1,0:T(8,128)}) %reduce-scatter.2.cloned.1.call-update) | async-done | bytes 524304 | tf_op jit(solution)/shard_map/reduce_scatter | solution.py:33
  500.8 2.2 fusion.2
  503.0 0.0 all-reduce.3.cloned.1.call-update
  503.0 0.8 fusion.9
  504.5 42.0 %all-reduce = (f32[]{:T(128)}, f32[256,41]{0,1:T(8,128)}) all-reduce(f32[]{:T(128)S(6)} %neg.3, f32[256,41]{0,1:T(8,128)S(1)} %fusion.9), channel_id=1, replica_groups=mesh['nodes'=32] {'nodes'}, use_global_device_ids=true, to_apply=%region_4.5 | all-reduce | flops 10497 | bytes 83976 | tf_op jit(solution)/shard_map/psum | solution.py:28
  547.9 88.6 %all-reduce.3.cloned.1.call-done = f32[602,256]{1,0:T(8,128)} async-done(((f32[602,256]{1,0:T(8,128)}), f32[602,256]{1,0:T(8,128)}) %all-reduce.3.cloned.1.call-update) | async-done | bytes 616464 | tf_op jit(solution)/shard_map/psum | solution.py:35
  636.5 1.9 copy.10
  (4 shorter events, 0.1 us)
Async XLA Ops:
  7.2 148.6 %all-gather.3.cloned.1.call-start = ((), (), s32[]{:S(2)}) async-start(), calls=%async_computation.1 | async-start | bytes 20545536 | tf_op jit(solution)/shard_map/all_gather | solution.py:17
  7.9 164.9 %copy-start.1 = (f32[602,256]{1,0:T(8,128)S(1)}, f32[602,256]{1,0:T(8,128)}, u32[]{:S(2)}) copy-start(f32[602,256]{1,0:T(8,128)} %param.8) | copy-start | bytes 1849348
  7.9 166.1 %copy-start.3 = (s32[512]{0:T(512)S(1)}, s32[512]{0:T(512)}, u32[]{:S(2)}) copy-start(s32[512]{0:T(512)} %param.11) | copy-start | bytes 6148
  7.9 242.0 %all-gather.5.cloned.1.call-start = ((), (), s32[]{:S(2)}) async-start(), calls=%async_computation.2 | async-start | bytes 8650752 | tf_op jit(solution)/shard_map/all_gather | solution.py:21
  173.9 326.9 %reduce-scatter.2.cloned.1.call-start = ((), (), s32[]{:S(2)}) async-start(), calls=%async_computation.3 | async-start | bytes 17301504 | tf_op jit(solution)/shard_map/reduce_scatter | solution.py:33
  174.0 88.7 %copy-start = (f32[256,41]{0,1:T(8,128)S(1)}, f32[256,41]{0,1:T(8,128)}, u32[]{:S(2)}) copy-start(f32[256,41]{0,1:T(8,128)} %param.9) | copy-start | bytes 125956
  174.0 88.9 %copy-start.2 = (s32[512]{0:T(512)S(1)}, s32[512]{0:T(512)}, u32[]{:S(2)}) copy-start(s32[512]{0:T(512)} %param.10) | copy-start | bytes 6148
  316.3 320.2 %all-reduce.3.cloned.1.call-start = ((), (), s32[]{:S(2)}) async-start(), calls=%async_computation.4 | async-start | bytes 1245184 | tf_op jit(solution)/shard_map/psum | solution.py:35
Sparse Core Ops, SparseCore 0:
  10.9 144.8 all-gather.2
  174.0 75.8 all-gather.4
  316.4 184.3 reduce-scatter.1
  506.5 130.0 all-reduce.2
where the time goes:
time: 648 us; the launch traced here: 646 us
  waiting for transfers between devices  498 us (77%)
  blocking collectives  80.5 us (12%)
  matrix products  48.2 us (7%)
  between operations  17 us (3%)
    reduce_scatter x1, waiting for transfers between devices, local_step(): lax.psum_scatter(part_sums, axis_name, scatter_dimension=0, tiled=True)  184 us
    all_gather x1, waiting for transfers between devices, local_step(): feats_all = lax.all_gather(feat_rows, axis_name, tiled=True)  148 us
    psum x1, waiting for transfers between devices, local_step(): lax.psum(lax.dot_general(agg_one, grad_one, ROW_CONTRACT, preferred_eleme...  88.6 us
    all_gather x1, waiting for transfers between devices, local_step(): hidden_all = lax.all_gather(hidden, axis_name, tiled=True)  75.9 us
    psum x1, blocking collectives, local_step(): lax.psum(-jnp.sum(weight * jnp.sum(onehot * log_prob, axis=-1)), axis_name)  42 us
    psum x1, blocking collectives, local_step(): label_count = lax.psum(jnp.sum(weight), axis_name)  38.5 us
    dot_general x1, matrix products, local_step(): jnp.dot(adj_rows, feats_all, preferred_element_type=jnp.float32)  17 us
    dot_general x1, matrix products, local_step(): lax.dot_general(adj_rows, back_two, ROW_CONTRACT, preferred_element_type=...  14.2 us
  transfers between devices with their start and end apart: 4, of which 4 were waited for; matrix products, arithmetic and copies ran while one was open for 0% of the time, Pallas kernels for 0%

commit v1 on v0

v1 whole, which is shorter than its diff:
```python
import functools

import jax
import jax.numpy as jnp
from jax import lax
from jax.experimental import pallas as pl
from jax.experimental.pallas import tpu as pltpu
from jax.sharding import PartitionSpec as P

AXIS = 'nodes'
MESH = pl.DeviceIdType.MESH
NN = (((1,), (0,)), ((), ()))
NT = (((1,), (1,)), ((), ()))
COL, CW, CCW, OA, OB, OZ = range(6)
VMEM_BYTES = 62 * 1024 * 1024


def _dot(a, b, dims=NN):
    return lax.dot_general(a, b, dims, preferred_element_type=jnp.float32)


def _ring(v):
    return v + v // 2 - 2 * (v // 3)


class _Geo:
    def __init__(self):
        self.me = lax.axis_index(AXIS)
        self.c = lax.rem(self.me, 2)
        chip = self.me // 2
        self.z = chip // 4
        self.r = _ring(lax.rem(chip, 4))
        self.nxt = lax.rem(self.r + 1, 4)
        self.prv = lax.rem(self.r + 3, 4)
        self.opp = lax.rem(self.r + 2, 4)
        self.other = 1 - self.c
        flip = self.z // 2
        zz = self.z + flip * (3 - 2 * self.z)
        first = 1 - zz
        self.k = [first + flip * (3 - 2 * first)] + [v + flip * (3 - 2 * v) for v in (2, 3)]

    def chip(self, z, r):
        return z * 4 + _ring(r)

    def dev(self, z, r, c):
        return self.chip(z, r) * 2 + c

    def away(self, z0):
        return self.z + 2 * (z0 < self.z).astype(jnp.int32) - 1

    def toward(self, z0):
        return self.z - 2 * (z0 < self.z).astype(jnp.int32) + 1


def _inside(z):
    return jnp.logical_and(z >= 0, z <= 3)


def _rcopy(src, dst, send_sem, recv_sem, dev):
    return pltpu.make_async_remote_copy(src_ref=src, dst_ref=dst, send_sem=send_sem, recv_sem=recv_sem, device_id=(dev,), device_id_type=MESH)


class _Sends:
    def __init__(self):
        self.pending = []

    def start(self, copy, cond=None):
        if cond is None:
            copy.start()
        else:
            @pl.when(cond)
            def _():
                copy.start()
        self.pending.append((copy, cond))

    def finish(self):
        for copy, cond in self.pending:
            if cond is None:
                copy.wait_send()
            else:
                @pl.when(cond)
                def _():
                    copy.wait_send()


def _barrier(g, far):
    sem = pltpu.get_barrier_semaphore()

    def signal(dev):
        pl.semaphore_signal(sem, inc=1, device_id=(dev,), device_id_type=MESH)

    for dev in (g.dev(g.z, g.r, g.other), g.dev(g.z, g.nxt, g.c), g.dev(g.z, g.prv, g.c)):
        signal(dev)
    if far:
        signal(g.dev(g.z, g.opp, g.c))
        for z0 in g.k:
            signal(g.dev(z0, g.r, g.c))
        pl.semaphore_wait(sem, 7)
    else:
        @pl.when(g.z < 3)
        def _():
            signal(g.dev(g.z + 1, g.r, g.c))

        @pl.when(g.z > 0)
        def _():
            signal(g.dev(g.z - 1, g.r, g.c))

        pl.semaphore_wait(sem, 5 - (g.z < 1).astype(jnp.int32) - (g.z > 2).astype(jnp.int32))


def _gather(g, buf, rows, unit, rsem, ssem, consume, early=None):
    ra = -(-rows * 5 // 32 // unit) * unit
    parts = {OA: (0, ra), OB: (ra, ra), OZ: (2 * ra, rows - 2 * ra)}
    ha = rows // 2 // unit * unit
    halves = {OA: (0, ha), OB: (ha, rows - ha)}
    z, r, c = g.z, g.r, g.c
    column = {COL: r, CW: g.prv, CCW: g.nxt, OA: g.opp, OB: g.opp, OZ: g.opp}
    sends = _Sends()

    def piece(kind, z0, core, same):
        ref = buf.at[g.dev(z0, column[kind], core)]
        if kind in (OA, OB):
            ref = ref.at[pl.ds(*(halves if same else parts)[kind]), :]
        elif kind == OZ:
            ref = ref.at[pl.ds(*parts[OZ]), :]
        return ref

    def recv(kind, z0, same=False, partner=False):
        core = g.other if partner else c
        ref = piece(kind, z0, core, same)
        sem = rsem.at[((1 if partner else 0) * 6 + kind) * 4 + z0]
        _rcopy(ref, ref, ssem.at[0], sem, g.me).wait_recv()

    def send(ref, kind, z0, slot, dev, cond=None, partner=False):
        sem = rsem.at[((1 if partner else 0) * 6 + kind) * 4 + z0]
        sends.start(_rcopy(ref, ref, ssem.at[slot * 4 + z0], sem, dev), cond)

    def to_partner(kind, z0, slot, same=False):
        send(piece(kind, z0, c, same), kind, z0, slot, g.dev(z, r, g.other), partner=True)

    def forward_col(z0):
        ref = piece(COL, z0, c, False)
        nz = g.away(z0)
        send(ref, COL, z0, 0, g.dev(nz, r, c), _inside(nz))
        send(ref, CW, z0, 2, g.dev(z, g.nxt, c))
        send(ref, CCW, z0, 3, g.dev(z, g.prv, c))
        to_partner(COL, z0, 4)

    def forward_sides(z0, same=False):
        sub = halves if same else parts
        send(piece(CW, z0, c, same).at[pl.ds(*sub[OA]), :], OA, z0, 5, g.dev(z, g.nxt, c))
        send(piece(CCW, z0, c, same).at[pl.ds(*sub[OB]), :], OB, z0, 7, g.dev(z, g.prv, c))
        to_partner(CW, z0, 6)
        to_partner(CCW, z0, 8)

    def take_opp(z0, same=False):
        kinds = ((OA, 9), (OB, 10)) + (() if same else ((OZ, 11),))
        if not same:
            recv(OZ, z0)
            nz = g.away(z0)
            send(piece(OZ, z0, c, False), OZ, z0, 12, g.dev(nz, r, c), _inside(nz))
            to_partner(OZ, z0, 11)
        for kind, slot in kinds[:2]:
            recv(kind, z0, same)
            to_partner(kind, z0, slot, same)

    def take_col(z0):
        recv(COL, z0)
        forward_col(z0)

    def take_sides(z0, same=False):
        recv(CW, z0, same)
        recv(CCW, z0, same)
        forward_sides(z0, same)

    def pair(kind, z0, same=False, wait_partner=True):
        if wait_partner:
            kinds = (kind,) if kind != OZ else ((OA, OB) if same else (OA, OB, OZ))
            for one in kinds:
                recv(one, z0, same, partner=True)
        consume(g.chip(z0, column[kind]))

    own = buf.at[g.me]
    send(own, COL, z, 0, g.dev(z + 1, r, c), z < 3)
    send(own, COL, z, 1, g.dev(z - 1, r, c), z > 0)
    send(own, CW, z, 2, g.dev(z, g.nxt, c))
    send(own, CCW, z, 3, g.dev(z, g.prv, c))
    send(own, COL, z, 4, g.dev(z, r, g.other), partner=True)
    if early is not None:
        early()
    k0, k1, k2 = g.k
    pair(COL, z)
    take_sides(z, True)
    take_col(k0)
    take_col(k1)
    pair(CW, z)
    pair(CCW, z)
    take_opp(z, True)
    oz = piece(OZ, z, c, False)
    late = g.away(k2)
    send(oz, OZ, z, 12, g.dev(2 * z - late, r, c), _inside(2 * z - late))
    pair(COL, k0)
    take_sides(k0)
    pair(COL, k1)
    take_col(k2)
    send(oz, OZ, z, 13, g.dev(late, r, c), _inside(late))
    pair(CW, k0)
    pair(CCW, k0)
    pair(OZ, z, True)
    take_sides(k1)
    pair(COL, k2)
    take_opp(k0)
    pair(CW, k1)
    pair(CCW, k1)
    take_sides(k2)
    pair(OZ, k0)
    take_opp(k1)
    pair(CW, k2)
    pair(CCW, k2)
    take_opp(k2)
    pair(OZ, k1)
    pair(OZ, k2)
    return sends


def _layer_one(nodes_block, feats, adj, own_x, w_one_t, s1_out, pos_out, h_out, cnt_out, a_v, x_all, acc, cnt, rsem, ssem, lsem):
    g = _Geo()
    load_x = pltpu.make_async_copy(own_x, x_all.at[g.me], lsem.at[0])
    load_a = pltpu.make_async_copy(adj, a_v, lsem.at[1])
    load_x.start()
    load_a.start()
    acc[...] = jnp.zeros_like(acc)
    cnt[...] = jnp.zeros_like(cnt)
    _barrier(g, False)
    load_x.wait()

    def consume(chip):
        def one(core, carry):
            b = chip * 2 + core
            a_blk = a_v[:, pl.ds(pl.multiple_of(b * nodes_block, nodes_block), nodes_block)]
            acc[...] += _dot(x_all[b], a_blk, NT)
            cnt[...] += x_all[b, pl.ds(feats // 16 * 16, 16), :].astype(jnp.float32)
            return carry

        lax.fori_loop(0, 2, one, 0)

    rows = x_all.shape[1]
    sends = _gather(g, x_all, rows, 16, rsem, ssem, consume, load_a.wait)
    s1 = acc[...].astype(jnp.bfloat16)
    s1_out[...] = s1
    pre = _dot(w_one_t[...], s1)
    pos_out[...] = jnp.where(pre > 0.0, 1.0, 0.0)
    h_out[...] = jnp.maximum(pre, 0.0).astype(jnp.bfloat16)
    row = lax.broadcasted_iota(jnp.int32, cnt.shape, 0) == feats % 16
    cnt_out[...] = jnp.broadcast_to(jnp.sum(jnp.where(row, cnt[...], 0.0), keepdims=True), cnt_out.shape)
    sends.finish()


def _layer_two(nodes_block, classes, adj, own_h, s1, pos, count, w_two_t, w_two, labels, mask, out,
               a_v, a_p, h_all, acc, ut, part, pa, pb, fl, fr, cz, oz, red, mine, got_l, got_z, quart,
               rsem, ssem, lsem, xsem, qrs, qss, trs, tss):
    g = _Geo()
    z, r, c = g.z, g.r, g.c
    k0, k1, k2 = g.k
    load_h = pltpu.make_async_copy(own_h, h_all.at[g.me], lsem.at[0])
    load_a = pltpu.make_async_copy(adj, a_v, lsem.at[1])
    load_h.start()
    load_a.start()
    acc[...] = jnp.zeros_like(acc)
    _barrier(g, True)
    load_h.wait()
    partner = g.dev(z, r, g.other)

    def cols(b):
        return pl.ds(pl.multiple_of(b * nodes_block, nodes_block), nodes_block)

    def swap(q):
        return _rcopy(adj.at[:, cols(q * 2 + g.other)], a_p.at[q], xsem.at[0], xsem.at[1], partner)

    def early():
        def one(q, carry):
            swap(q).start()
            return carry

        lax.fori_loop(0, 16, one, 0)
        load_a.wait()

    def consume(chip):
        def one(core, carry):
            b = chip * 2 + core
            acc[...] += _dot(h_all[b], a_v[:, cols(b)], NT)
            return carry

        lax.fori_loop(0, 2, one, 0)

    hidden = h_all.shape[1]
    sends = _gather(g, h_all, hidden, 16, rsem, ssem, consume, early)

    s2 = acc[...].astype(jnp.bfloat16)
    logits = _dot(w_two_t[...], s2)
    weight = mask[...].astype(jnp.float32)
    onehot = (labels[...] == lax.broadcasted_iota(jnp.int32, logits.shape, 0)).astype(jnp.float32)
    shifted = logits - jnp.max(logits, axis=0, keepdims=True)
    log_prob = shifted - jnp.log(jnp.sum(jnp.exp(shifted), axis=0, keepdims=True))
    g2 = (weight * (jnp.exp(log_prob) - onehot) / count[0:1, 0:1]).astype(jnp.bfloat16)
    ut[0] = _dot(w_two[...], g2).astype(jnp.bfloat16)
    send_u = _rcopy(ut.at[0], ut.at[1], xsem.at[2], xsem.at[3], partner)
    send_u.start()
    loss = -jnp.sum(weight * jnp.sum(onehot * log_prob, axis=0, keepdims=True), keepdims=True)
    feats_rows = s1.shape[0]
    extra = red.shape[0] - feats_rows
    dw2 = _dot(g2, s2, NT)
    red[pl.ds(feats_rows, classes), :] = dw2
    red[pl.ds(feats_rows + classes, extra - classes), :] = jnp.broadcast_to(loss, (extra - classes, hidden))
    _rcopy(a_p, a_p, xsem.at[0], xsem.at[1], partner).wait_recv()
    send_u.wait_recv()

    def make(z0, column):
        q = g.chip(z0, column)
        part[q] = _dot(ut[0], a_v[:, cols(q * 2 + c)]) + _dot(ut[1], a_p[q])

    ra = -(-hidden * 5 // 32 // 8) * 8
    parts = {OA: (0, ra), OB: (ra, ra), OZ: (2 * ra, hidden - 2 * ra)}
    halves = {OA: (0, hidden // 2), OB: (hidden // 2, hidden // 2)}
    rs = _Sends()

    def rsend(src, dst, slot, index, recv_index, dev, cond=None):
        rs.start(_rcopy(src, dst, qss.at[slot * 4 + index], qrs.at[recv_index], dev), cond)

    def rwait(ref, index):
        _rcopy(ref, ref, qss.at[0], qrs.at[index], g.me).wait_recv()

    def out_opp(z0, same=False):
        sub = halves if same else parts
        blk = part.at[g.chip(z0, g.opp)]
        rsend(blk.at[pl.ds(*sub[OA]), :], pa.at[z0, pl.ds(0, sub[OA][1]), :], 0, z0, z0, g.dev(z, g.prv, c))
        rsend(blk.at[pl.ds(*sub[OB]), :], pb.at[z0, pl.ds(0, sub[OB][1]), :], 1, z0, 4 + z0, g.dev(z, g.nxt, c))

    def slot_at(z0, nz):
        end = (nz == z0).astype(jnp.int32) * (nz < z).astype(jnp.int32)
        return z0 + end * (4 - z0)

    def out_opp_z(z0):
        blk = part.at[g.chip(z0, g.opp), pl.ds(*parts[OZ]), :]
        far = g.away(z0)

        @pl.when(_inside(far))
        def _():
            rwait(oz.at[z0], 21 + z0)
            q = g.chip(z0, g.opp)
            part[q, pl.ds(*parts[OZ]), :] += oz[z0]

        nz = g.toward(z0)
        slot = slot_at(z0, nz)
        rsend(blk, oz.at[slot], 2, z0, 21 + slot, g.dev(nz, r, c))

    def out_sides(z0, same=False):
        sub = halves if same else parts
        qp, qn = g.chip(z0, g.prv), g.chip(z0, g.nxt)
        na, nb = sub[OA][1], sub[OB][1]
        rwait(pa.at[z0, pl.ds(0, na), :], z0)
        part[qp, pl.ds(*sub[OA]), :] += pa[z0, pl.ds(0, na), :]
        rsend(part.at[qp], fr.at[z0], 3, z0, 12 + z0, g.dev(z, g.prv, c))
        rwait(pb.at[z0, pl.ds(0, nb), :], 4 + z0)
        part[qn, pl.ds(*sub[OB]), :] += pb[z0, pl.ds(0, nb), :]
        rsend(part.at[qn], fl.at[z0], 4, z0, 8 + z0, g.dev(z, g.nxt, c))

    def add_sides(z0):
        q = g.chip(z0, r)
        rwait(fl.at[z0], 8 + z0)
        rwait(fr.at[z0], 12 + z0)
        part[q] += fl[z0] + fr[z0]

    def add_cz(slot, z0, cond):
        @pl.when(cond)
        def _():
            rwait(cz.at[slot], 16 + slot)
            part[g.chip(z0, r)] += cz[slot]

    def out_col(z0):
        add_sides(z0)
        add_cz(z0, z0, _inside(g.away(z0)))
        nz = g.toward(z0)
        slot = slot_at(z0, nz)
        rsend(part.at[g.chip(z0, r)], cz.at[slot], 5, z0, 16 + slot, g.dev(nz, r, c))

    make(k2, g.opp)
    out_opp(k2)
    make(k1, g.opp)
    out_opp(k1)
    make(k2, g.prv)
    make(k2, g.nxt)
    out_opp_z(k2)
    out_sides(k2)
    make(k0, g.opp)
    out_opp(k0)
    make(k1, g.prv)
    make(k1, g.nxt)
    out_opp_z(k1)
    out_sides(k1)
    make(k2, r)
    make(k0, g.prv)
    make(k0, g.nxt)
    out_opp_z(k0)
    out_sides(k0)
    out_col(k2)
    for column in (g.opp, g.prv, g.nxt, r):
        make(z, column)
    make(k1, r)
    make(k0, r)
    out_col(k1)

    def add_oz(slot, cond):
        @pl.when(cond)
        def _():
            rwait(oz.at[slot], 21 + slot)
            part[g.chip(z, g.opp), pl.ds(*parts[OZ]), :] += oz[slot]

    add_oz(z, z > 0)
    add_oz(4, z < 3)
    out_opp(z, True)
    out_col(k0)
    out_sides(z, True)
    add_sides(z)
    add_cz(z, z, z > 0)
    add_cz(4, z, z < 3)
    d_hidden = part[g.chip(z, r)]
    g1 = jnp.where(pos[...] > 0.0, d_hidden, 0.0).astype(jnp.bfloat16)
    red[pl.ds(0, feats_rows), :] = _dot(s1[...], g1, NT)

    half = hidden // 2
    rows = red.shape[0]
    quarter = rows // 4
    tail = _Sends()

    def tsend(src, dst, index, dev):
        tail.start(_rcopy(src, dst, tss.at[index], trs.at[index], dev))

    def twait(ref, index):
        _rcopy(ref, ref, tss.at[0], trs.at[index], g.me).wait_recv()

    def lanes(core):
        return pl.ds(pl.multiple_of(core * half, half), half)

    def band(place):
        return pl.ds(pl.multiple_of(place * quarter, 8), quarter)

    tsend(red.at[:, lanes(g.other)], mine.at[1], 0, partner)
    twait(mine.at[1], 0)
    mine[0] = red[:, lanes(c)] + mine[1]
    peers = (g.nxt, g.prv, g.opp)
    for i, place in enumerate(peers):
        tsend(mine.at[0, band(place), :], got_l.at[i], 1 + i, g.dev(z, place, c))
    total = mine[0, band(r), :]
    for i in range(3):
        twait(got_l.at[i], 1 + i)
        total = total + got_l[i]
    quart[...] = total
    for i, z0 in enumerate((k0, k1, k2)):
        tail.start(_rcopy(quart, got_z.at[z], tss.at[4 + i], trs.at[4 + z], g.dev(z0, r, c)))
    got_z[z] = quart[...]
    for z0 in g.k:
        twait(got_z.at[z0], 4 + z0)
    out_lanes = out.at[:, lanes(c)]
    final = out_lanes.at[band(r), :]
    out[band(r), lanes(c)] = (got_z[0] + got_z[1]) + (got_z[2] + got_z[3])
    for i, place in enumerate(peers):
        tail.start(_rcopy(final, final, tss.at[8 + i], trs.at[8 + r], g.dev(z, place, c)))
    for place in peers:
        twait(out_lanes.at[band(place), :], 8 + place)
    tail.start(_rcopy(out_lanes, out_lanes, tss.at[12], trs.at[12], partner))
    other = out.at[:, lanes(g.other)]
    twait(other, 12)

    swap_all = _rcopy(a_p, a_p, xsem.at[0], xsem.at[1], partner)
    swap_all.wait_send()
    send_u.wait_send()
    sends.finish()
    rs.finish()
    tail.finish()


def solution(mesh):
    def local_step(adj_rows, feat_rows, w_one, w_two, label_rows, mask_rows):
        block, feats = feat_rows.shape
        hidden, classes = w_two.shape
        devices = mesh.shape[AXIS]
        nodes = adj_rows.shape[1]
        bf16, f32 = jnp.bfloat16, jnp.float32
        pad = -(-(feats + 1) // 16) * 16
        vmem = pl.BlockSpec(memory_space=pltpu.VMEM)
        anywhere = pl.BlockSpec(memory_space=pl.ANY)
        dma = pltpu.SemaphoreType.DMA

        own_x = jnp.concatenate([feat_rows.T, mask_rows.astype(bf16)[None, :], jnp.zeros((pad - feats - 1, block), bf16)], axis=0)
        w_one_t = jnp.concatenate([w_one.astype(bf16).T, jnp.zeros((hidden, pad - feats), bf16)], axis=1)
        s1, pos, h1, count = pl.pallas_call(
            functools.partial(_layer_one, block, feats),
            out_shape=(jax.ShapeDtypeStruct((pad, block), bf16), jax.ShapeDtypeStruct((hidden, block), f32),
                       jax.ShapeDtypeStruct((hidden, block), bf16), jax.ShapeDtypeStruct((8, 128), f32)),
            in_specs=[anywhere, anywhere, vmem],
            out_specs=(vmem, vmem, vmem, vmem),
            scratch_shapes=[
                pltpu.VMEM((block, nodes), bf16), pltpu.VMEM((devices, pad, block), bf16),
                pltpu.VMEM((pad, block), f32), pltpu.VMEM((16, block), f32),
                dma((48,)), dma((56,)), dma((2,)),
            ],
            compiler_params=pltpu.CompilerParams(collective_id=0, has_side_effects=True, vmem_limit_bytes=VMEM_BYTES),
            name='layer_one',
        )(adj_rows, own_x, w_one_t)

        weight_two = w_two.astype(bf16)
        red_rows = -(-(pad + classes + 1) // 32) * 32
        quarter = red_rows // 4
        ra = -(-hidden * 5 // 32 // 8) * 8
        out = pl.pallas_call(
            functools.partial(_layer_two, block, classes),
            out_shape=jax.ShapeDtypeStruct((red_rows, hidden), f32),
            in_specs=[anywhere, anywhere] + [vmem] * 7,
            out_specs=vmem,
            scratch_shapes=[
                pltpu.VMEM((block, nodes), bf16), pltpu.VMEM((16, block, block), bf16),
                pltpu.VMEM((devices, hidden, block), bf16), pltpu.VMEM((hidden, block), f32),
                pltpu.VMEM((2, hidden, block), bf16), pltpu.VMEM((16, hidden, block), f32),
                pltpu.VMEM((4, hidden // 2, block), f32), pltpu.VMEM((4, hidden // 2, block), f32),
                pltpu.VMEM((4, hidden, block), f32), pltpu.VMEM((4, hidden, block), f32),
                pltpu.VMEM((5, hidden, block), f32), pltpu.VMEM((5, hidden - 2 * ra, block), f32),
                pltpu.VMEM((red_rows, hidden), f32), pltpu.VMEM((2, red_rows, hidden // 2), f32),
                pltpu.VMEM((3, quarter, hidden // 2), f32), pltpu.VMEM((4, quarter, hidden // 2), f32),
                pltpu.VMEM((quarter, hidden // 2), f32),
                dma((48,)), dma((56,)), dma((2,)), dma((4,)), dma((26,)), dma((24,)), dma((13,)), dma((13,)),
            ],
            compiler_params=pltpu.CompilerParams(collective_id=1, has_side_effects=True, vmem_limit_bytes=VMEM_BYTES),
            name='layer_two',
        )(adj_rows, h1, s1, pos, count, weight_two.T, weight_two, label_rows[None, :], mask_rows[None, :])

        dw_one = out[:feats]
        dw_two = out[pad:pad + classes].T
        loss = out[pad + classes, 0:1] / count[0, 0:1]
        return loss, dw_one, dw_two

    return jax.shard_map(local_step, mesh=mesh, in_specs=(P(AXIS, None), P(AXIS, None), P(None, None), P(None, None), P(AXIS), P(AXIS)), out_specs=(P(None), P(None, None), P(None, None)), check_vma=False)
```

time: 648 us -> 245 us (0.38)
  waiting for transfers between devices: 498 us -> 0 us
  Pallas kernels: 0 us -> 232 us
  blocking collectives: 80.5 us -> 0 us
  matrix products: 48.2 us -> 0 us
  between operations: 17 us -> 3.16 us
    pallas_call x0 -> x2, Pallas kernels: none -> 232 us  [the longest x1 137 us: local_step(): pl.pallas_call(functools.partial(_layer_two, block, classes), out_shape=j...]
    all_gather x2 -> x0, waiting for transfers between devices: 224 us -> none  [the longest x1 148 us: local_step(): feats_all = lax.all_gather(feat_rows, axis_name, tiled=True)]
    reduce_scatter x1 -> x0, waiting for transfers between devices: 184 us -> none  [local_step(): lax.psum_scatter(part_sums, axis_name, scatter_dimension=0, tiled=True)]
    psum x1 -> x0, waiting for transfers between devices: 88.6 us -> none  [local_step(): lax.psum(lax.dot_general(agg_one, grad_one, ROW_CONTRACT, preferred_eleme...]
    psum x2 -> x0, blocking collectives: 80.5 us -> none  [the longest x1 42 us: local_step(): lax.psum(-jnp.sum(weight * jnp.sum(onehot * log_prob, axis=-1)), axis_name)]
    dot_general x7 -> x0, matrix products: 48.2 us -> none  [the longest x1 17 us: local_step(): jnp.dot(adj_rows, feats_all, preferred_element_type=jnp.float32)]
  transfers between devices with their start and end apart: 4 -> 0, of which waited for: 4 -> 0; matrix products, arithmetic and copies ran while one was open for 0% -> 0% of each run, Pallas kernels for 0% -> 0%
where the time goes in v1:
time: 245 us
  Pallas kernels  232 us (95%)
  local copies, waits for them, and re-layouts  7.63 us (3%)
  between operations  3.16 us (1%)
    pallas_call x1, Pallas kernels, local_step(): pl.pallas_call(functools.partial(_layer_two, block, classes), out_shape=j...  137 us
    pallas_call x1, Pallas kernels, local_step(): pl.pallas_call(functools.partial(_layer_one, block, feats), out_shape=(ja...  94.7 us

profile of v1, /device:TPU:1, one launch (start us, length us, event | category | flops | bytes accessed | tf_op | source)
XLA Modules:
  0.0 244.5 jit_solution(3443049062401093356)
XLA Ops:
  0.6 0.0 copy-start.3
  0.6 0.0 copy-start
  0.7 1.2 convert_element_type.10
  1.8 0.2 copy.12
  2.0 0.7 concatenate.7.w_one_t
  2.8 0.0 copy-done.3
  2.8 0.1 pad.3.clone
  2.9 0.0 copy-done
  2.9 1.0 maximum_maximum_fusion.own_x
  3.9 0.0 copy-start.2
  3.9 94.7 %layer_one.1 = (bf16[608,512]{1,0:T(8,128)(2,1)}, f32[256,512]{1,0:T(8,128)}, bf16[256,512]{1,0:T(8,128)(2,1)}, f32[8,128]{1,0:T(8,128)}) custom-call(bf16[512,16384]{1,0:T(8,128)(2,1)} %adj.3, bf16[608,512]{1,0:T(8,128)(2,1)} %maximum_maximum_fusion.own_x, bf16[256,608]{1,0:T(8,128)(2,1)} %concatenate.7.w_one_t), custom_call_target="tpu_custom_call" | custom-call | tf_op jit(solution)/shard_map/layer_one/pallas_call | solution.py:497
  98.7 0.0 copy-done.2
  98.7 0.1 copy.13.w_two
  98.8 0.0 copy-start.1
  98.8 0.7 copy.14.w_two_t
  99.5 0.0 copy-done.1
  99.5 136.8 %layer_two.1 = f32[672,256]{1,0:T(8,128)} custom-call(bf16[512,16384]{1,0:T(8,128)(2,1)} %adj.3, bf16[256,512]{1,0:T(8,128)(2,1)} %get-tuple-element.7.own_h, bf16[608,512]{1,0:T(8,128)(2,1)} %get-tuple-element.8.s1, f32[256,512]{1,0:T(8,128)} %get-tuple-element.9.pos, f32[8,128]{1,0:T(8,128)} %get-tuple-element.10.count, bf16[41,256]{1,0:T(8,128)(2,1)} %copy.14.w_two_t, ...), custom_call_target="tpu_custom_call" | custom-call | tf_op jit(solution)/shard_map/layer_two/pallas_call | solution.py:516
  236.3 1.2 slice.12
  237.5 1.2 slice.13
  240.0 1.9 slice.14
  242.0 1.4 slice_bitcast_fusion
  (3 shorter events, 0.0 us)
Async XLA Ops:
  0.6 2.2 copy-start.3
  0.6 2.2 copy-start
  3.9 94.8 %copy-start.2 = (f32[256,41]{0,1:T(8,128)S(1)}, f32[256,41]{0,1:T(8,128)}, u32[]{:S(2)}) copy-start(f32[256,41]{0,1:T(8,128)} %param.9) | copy-start | bytes 125956
  98.8 0.7 copy-start.1
